TPU v7x, 32 devices: a whole 2x2x4 slice. The times are simulated.
32 devices in a mesh: row: 16 (over z, y, core), col: 2 (over x).
Axes of the slice: x: 2, y: 2, z: 4, core: 2. Of those that a mesh axis runs over, the one named last changes fastest.
Arguments:
- diag_tile: float32 [1024, 1024], P(('row', 'col')), as said below
- left_row: bfloat16 [1024, 32, 256], P('col', 'row'), may hold values from -0.3984375 to 0.3984375
- right_row: bfloat16 [1024, 32, 256], P('col', 'row'), may hold values from -1.09375 to 1.09375
- right_col: bfloat16 [1024, 8, 256], P('row', 'col'), may hold values from -1.09375 to 1.09375
- bucket_row: int32 [32], P('row'), may hold values from 1 to 4
- bucket_col: int32 [8], P('col'), may hold values from 1 to 4
Outputs:
- panel_row: bfloat16 [1024, 32, 256], P('col', 'row')
- panel_col: bfloat16 [1024, 8, 256], P('row', 'col')
- update_left: bfloat16 [32, 8, 1024, 256], P('row', 'col')
Inputs may be any that keep to these rules, and one draw needn't show every extreme that they name: diag_tile is symmetric positive definite. `bucket_row`: a tile's rank is 64 times its bucket; factor columns from the rank on are not part of the tile. `bucket_col`: as for bucket_row.
All inputs are finite; a program needn't handle non-finite values.
Results may differ from a plain program's by a relative error of at most 0.0062.
Values may be sent and summed in bfloat16 or wider, within the bound.
A program may use at most 128 MiB of HBM per device.

v0:
```python
import jax
import jax.numpy as jnp
from jax import lax
from jax.sharding import PartitionSpec as P

RSTEP = 64


def mask_columns(right, bucket):
    live = jnp.arange(right.shape[2], dtype=jnp.int32)[None, :] < (RSTEP * bucket)[:, None]
    return jnp.where(live[None, :, :], right, jnp.zeros_like(right))


def solve_whole(inverse, gathered):
    flat = gathered.astype(jnp.float32).reshape(gathered.shape[0], -1)
    solved = jnp.dot(
        inverse, flat, precision=lax.Precision.HIGHEST, preferred_element_type=jnp.float32
    )
    return solved.astype(jnp.bfloat16).reshape(gathered.shape)


def per_device(diag_tile, left_row, right_row, right_col, bucket_row, bucket_col):
    whole_tile = lax.all_gather(diag_tile, ("row", "col"), axis=0, tiled=True)
    order = whole_tile.shape[0]
    lower_factor = jnp.linalg.cholesky(whole_tile)
    identity = jnp.eye(order, dtype=jnp.float32)
    inverse = lax.linalg.triangular_solve(lower_factor, identity, left_side=True, lower=True)
    masked_row = mask_columns(right_row, bucket_row)
    masked_col = mask_columns(right_col, bucket_col)
    row_position = lax.axis_index("col")
    col_position = lax.axis_index("row")
    full_row = solve_whole(inverse, lax.all_gather(masked_row, "col", axis=0, tiled=True))
    full_col = solve_whole(inverse, lax.all_gather(masked_col, "row", axis=0, tiled=True))
    panel_row = lax.dynamic_slice_in_dim(
        full_row, row_position * masked_row.shape[0], masked_row.shape[0], 0
    )
    panel_col = lax.dynamic_slice_in_dim(
        full_col, col_position * masked_col.shape[0], masked_col.shape[0], 0
    )
    coupling = jnp.einsum(
        "kia,kjb->ijab", full_row, full_col, preferred_element_type=jnp.float32
    ).astype(jnp.bfloat16)
    update = jnp.einsum(
        "kia,ijab->ijkb",
        lax.all_gather(left_row, "col", axis=0, tiled=True),
        coupling,
        preferred_element_type=jnp.float32,
    )
    update_left = (-update).astype(jnp.bfloat16)
    return (panel_row, panel_col, update_left)


def solution(mesh):
    return jax.shard_map(
        per_device,
        mesh=mesh,
        in_specs=(
            P(("row", "col"), None),
            P("col", "row", None),
            P("col", "row", None),
            P("row", "col", None),
            P("row"),
            P("col"),
        ),
        out_specs=(P("col", "row", None), P("row", "col", None), P("row", "col", None, None)),
        check_vma=False,
    )
```

profile of v0, /device:TPU:0, one launch (start us, length us, event | category | flops | bytes accessed | tf_op | source)
XLA Modules:
  0.0 521.5 jit_solution(5907188996161533663)
XLA Ops:
  19.1 15.3 %all-gather.7.cloned.1.call-done = bf16[1024,2,256]{2,1,0:T(2,128)(2,1)} async-done(((bf16[512,2,256]{2,1,0:T(2,128)(2,1)}), bf16[1024,2,256]{2,1,0:T(2,128)(2,1)}) %all-gather.7.cloned.1.call-update) | async-done | bytes 1048592 | tf_op jit(solution)/shard_map/all_gather | solution.py:32
  34.4 2.5 copy.24
  36.9 41.7 %all-gather.9.cloned.1.call-done = bf16[1024,4,256]{2,1,0:T(4,128)(2,1)} async-done(((bf16[64,4,256]{2,1,0:T(4,128)(2,1)}), bf16[1024,4,256]{2,1,0:T(4,128)(2,1)}) %all-gather.9.cloned.1.call-update) | async-done | bytes 2097168 | tf_op jit(solution)/shard_map/all_gather | solution.py:33
  80.7 61.4 %all-gather.5.cloned.1.call-done = f32[1024,1024]{1,0:T(8,128)} async-done(((f32[32,1024]{1,0:T(8,128)}), f32[1024,1024]{1,0:T(8,128)}) %all-gather.5.cloned.1.call-update) | async-done | bytes 4194320 | tf_op jit(solution)/shard_map/all_gather | solution.py:23
  142.1 5.8 %copy.15 = f32[1024,1024]{0,1:T(8,128)} copy(f32[1024,1024]{1,0:T(8,128)} %all-gather.5.cloned.1.call-done) | data formatting | bytes 8388608 | tf_op jit(solution)/shard_map/all_gather | solution.py:23
  147.9 4.8 fusion.1
  154.7 11.7 %cholesky.223 = f32[128,128]{1,0:T(8,128)S(1)} custom-call(f32[128,128]{1,0:T(8,128)S(1)} %cholesky.580), custom_call_target="Cholesky" | custom-call | tf_op jit(solution)/shard_map/jit(cholesky)/cholesky | solution.py:25
  166.4 9.8 %custom-call.62 = f32[1,128,128]{1,2,0:T(8,128)S(1)} custom-call(f32[1,128,128]{2,1,0:T(8,128)S(1)} %get-tuple-element.73), custom_call_target="InvertDiagBlocksLowerTriangular" | custom-call | tf_op jit(solution)/shard_map/jit(cholesky)/cholesky | solution.py:25
  176.2 2.5 cholesky.255
  182.6 11.9 %cholesky.244 = f32[128,128]{1,0:T(8,128)S(1)} custom-call(f32[128,128]{1,0:T(8,128)S(1)} %cholesky.584), custom_call_target="Cholesky" | custom-call | tf_op jit(solution)/shard_map/jit(cholesky)/cholesky | solution.py:25
  195.2 9.8 %custom-call.63 = f32[1,128,128]{1,2,0:T(8,128)S(1)} custom-call(f32[1,128,128]{2,1,0:T(8,128)S(1)} %get-tuple-element.70), custom_call_target="InvertDiagBlocksLowerTriangular" | custom-call | tf_op jit(solution)/shard_map/jit(cholesky)/cholesky | solution.py:25
  208.3 11.7 %cholesky.468 = f32[128,128]{1,0:T(8,128)S(1)} custom-call(f32[128,128]{1,0:T(8,128)S(1)} %cholesky.589), custom_call_target="Cholesky" | custom-call | tf_op jit(solution)/shard_map/jit(cholesky)/cholesky | solution.py:25
  221.3 9.8 %custom-call.64 = f32[1,128,128]{1,2,0:T(8,128)S(1)} custom-call(f32[1,128,128]{2,1,0:T(8,128)S(1)} %get-tuple-element.67), custom_call_target="InvertDiagBlocksLowerTriangular" | custom-call | tf_op jit(solution)/shard_map/jit(cholesky)/cholesky | solution.py:25
  234.6 11.9 %cholesky.487 = f32[128,128]{1,0:T(8,128)S(1)} custom-call(f32[128,128]{1,0:T(8,128)S(1)} %cholesky.594), custom_call_target="Cholesky" | custom-call | tf_op jit(solution)/shard_map/jit(cholesky)/cholesky | solution.py:25
  247.7 9.8 %custom-call.65 = f32[1,128,128]{1,2,0:T(8,128)S(1)} custom-call(f32[1,128,128]{2,1,0:T(8,128)S(1)} %get-tuple-element.64), custom_call_target="InvertDiagBlocksLowerTriangular" | custom-call | tf_op jit(solution)/shard_map/jit(cholesky)/cholesky | solution.py:25
  261.0 11.7 %cholesky.506 = f32[128,128]{1,0:T(8,128)S(1)} custom-call(f32[128,128]{1,0:T(8,128)S(1)} %cholesky.599), custom_call_target="Cholesky" | custom-call | tf_op jit(solution)/shard_map/jit(cholesky)/cholesky | solution.py:25
  274.0 10.2 %custom-call.66 = f32[1,128,128]{1,2,0:T(8,128)S(1)} custom-call(f32[1,128,128]{2,1,0:T(8,128)S(1)} %get-tuple-element.61), custom_call_target="InvertDiagBlocksLowerTriangular" | custom-call | tf_op jit(solution)/shard_map/jit(cholesky)/cholesky | solution.py:25
  287.4 11.7 %cholesky.526 = f32[128,128]{1,0:T(8,128)S(1)} custom-call(f32[128,128]{1,0:T(8,128)S(1)} %cholesky.604), custom_call_target="Cholesky" | custom-call | tf_op jit(solution)/shard_map/jit(cholesky)/cholesky | solution.py:25
  300.5 9.8 %custom-call.67 = f32[1,128,128]{1,2,0:T(8,128)S(1)} custom-call(f32[1,128,128]{2,1,0:T(8,128)S(1)} %get-tuple-element.58), custom_call_target="InvertDiagBlocksLowerTriangular" | custom-call | tf_op jit(solution)/shard_map/jit(cholesky)/cholesky | solution.py:25
  313.3 11.9 %cholesky.546 = f32[128,128]{1,0:T(8,128)S(1)} custom-call(f32[128,128]{1,0:T(8,128)S(1)} %cholesky.609), custom_call_target="Cholesky" | custom-call | tf_op jit(solution)/shard_map/jit(cholesky)/cholesky | solution.py:25
  326.4 9.8 %custom-call.68 = f32[1,128,128]{1,2,0:T(8,128)S(1)} custom-call(f32[1,128,128]{2,1,0:T(8,128)S(1)} %get-tuple-element.55), custom_call_target="InvertDiagBlocksLowerTriangular" | custom-call | tf_op jit(solution)/shard_map/jit(cholesky)/cholesky | solution.py:25
  338.9 11.7 %cholesky.564 = f32[128,128]{1,0:T(8,128)S(1)} custom-call(f32[128,128]{1,0:T(8,128)S(1)} %convolution_subtract_fusion.11), custom_call_target="Cholesky" | custom-call | tf_op jit(solution)/shard_map/jit(cholesky)/cholesky | solution.py:25
  357.4 4.9 select_select_fusion
  362.3 23.2 %while.1 = (s32[]{:T(128)}, f32[1024,1024]{1,0:T(8,128)}, s32[8,2]{0,1:T(2,128)S(1)}, f32[8,128,128]{2,1,0:T(8,128)S(1)}, s32[]{:T(128)}) while((s32[]{:T(128)}, f32[1024,1024]{1,0:T(8,128)}, s32[8,2]{0,1:T(2,128)S(1)}, f32[8,128,128]{2,1,0:T(8,128)S(1)}, s32[]{:T(128)}) %tuple.63), condition=%wide.while_cond, body=%wide.while_body.sunk | while | flops 2 | bytes 131181 | solution.py:27
  385.5 78.8 %custom-call.69 = f32[8,128,128]{1,2,0:T(8,128)S(1)} custom-call(f32[8,128,128]{2,1,0:T(8,128)S(1)} %get-tuple-element.10), custom_call_target="InvertDiagBlocksLowerTriangular" | custom-call | tf_op jit(solution)/shard_map/triangular_solve | solution.py:27
  476.4 2.6 convolution_subtract_fusion.2
  479.7 2.8 convolution_subtract_fusion.1
  483.2 3.5 convolution_subtract_fusion.3
  487.4 3.6 convolution_convert_fusion.2
  490.9 8.2 %convolution_convert_fusion = bf16[1024,1024]{0,1:T(8,128)(2,1)} fusion(f32[1024,1024]{1,0:T(8,128)S(1)} %convolution_dynamic-update-slice_fusion, bf16[1024,1024]{1,0:T(8,128)(2,1)S(1)} %bitcast.130), kind=kOutput, calls=%fused_computation.17 | convolution fusion | flops 12885950464 | bytes 8388608 | tf_op jit(solution)/shard_map/dot_general | solution.py:16
  499.1 6.2 %fusion = bf16[2,4,1024,256]{2,3,1,0:T(8,128)(2,1)} fusion(bf16[1024,4,256,1]{0,2,1,3:T(8,128)(2,1)} %bitcast.136, bf16[1024,2,256,1]{0,2,3,1:T(8,128)(2,1)S(1)} %bitcast.134, bf16[1024,2,256]{2,0,1:T(8,128)(2,1)} %all-gather.11.cloned.1.call-done), kind=kOutput, calls=%fused_computation.4 | convolution fusion | flops 2152202240 | bytes 8388608 | tf_op jit(solution)/shard_map/kia,ijab->ijkb/dot_general | solution.py:43
  505.3 6.2 %copy.19 = bf16[2,4,1024,256]{3,2,1,0:T(8,128)(2,1)} copy(bf16[2,4,1024,256]{2,3,1,0:T(8,128)(2,1)} %fusion) | data formatting | bytes 8388608
  (104 shorter events, 87.9 us)
Async XLA Ops:
  7.2 27.2 %all-gather.7.cloned.1.call-start = ((), (), s32[]{:S(2)}) async-start(), calls=%async_computation.1 | async-start | bytes 1572864 | tf_op jit(solution)/shard_map/all_gather | solution.py:32
  10.2 68.4 %all-gather.9.cloned.1.call-start = ((), (), s32[]{:S(2)}) async-start(), calls=%async_computation.2 | async-start | bytes 2228224 | tf_op jit(solution)/shard_map/all_gather | solution.py:33
  12.6 129.4 %all-gather.5.cloned.1.call-start = ((), (), s32[]{:S(2)}) async-start(), calls=%async_computation | async-start | bytes 4325376 | tf_op jit(solution)/shard_map/all_gather | solution.py:23
  13.4 485.7 %all-gather.11.cloned.1.call-start = ((), (), s32[]{:S(2)}) async-start(), calls=%async_computation.3 | async-start | bytes 1572864 | tf_op jit(solution)/shard_map/all_gather | solution.py:45
  152.7 2.0 copy-start.1
  464.3 3.9 copy-start
  482.5 4.8 copy-start.2
Sparse Core Ops, SparseCore 0:
  10.3 23.9 all-gather.6
  37.1 41.4 all-gather.8
  81.6 60.4 all-gather.4
  143.5 20.0 all-gather.10
where the time goes:
time: 525 us; the launch traced here: 521 us
  other arithmetic  270 us (51%)
  waiting for transfers between devices  119 us (23%)
  matrix products  63.7 us (12%)
  local copies, waits for them, and re-layouts  49.1 us (9%)
  between operations  19.4 us (4%)
    another operation x30, other arithmetic, per_device(): lower_factor = jnp.linalg.cholesky(whole_tile)  172 us
    another operation x3, other arithmetic, per_device(): lax.linalg.triangular_solve(lower_factor, identity, left_side=True, lower...  83.7 us
    all_gather x1, waiting for transfers between devices, per_device(): whole_tile = lax.all_gather(diag_tile, ('row', 'col'), axis=0, tiled=True)  61.4 us
    all_gather x1, waiting for transfers between devices, per_device(): lax.all_gather(masked_col, 'row', axis=0, tiled=True)  41.7 us
    another operation x24, local copies, waits for them, and re-layouts  23 us
    another operation x14, matrix products, per_device(): lower_factor = jnp.linalg.cholesky(whole_tile)  23 us
    another operation x15, matrix products, per_device(): lax.linalg.triangular_solve(lower_factor, identity, left_side=True, lower...  22.9 us
    unnamed x12, local copies, waits for them, and re-layouts  16.6 us
  transfers between devices with their start and end apart: 4, of which 3 were waited for; matrix products, arithmetic and copies ran while one was open for 69% of the time, Pallas kernels for 0%

commit v1 on v0

--- a/solution.py
+++ b/solution.py
@@ -1,9 +1,133 @@
+import functools
+
 import jax
 import jax.numpy as jnp
 from jax import lax
+from jax.experimental import pallas as pl
+from jax.experimental.pallas import tpu as pltpu
 from jax.sharding import PartitionSpec as P
 
 RSTEP = 64
+BLOCK = 128
+SUB = 8
+HI = lax.Precision.HIGHEST
+
+
+def dot_nn(a, b):
+    return lax.dot_general(a, b, (((1,), (0,)), ((), ())), precision=HI, preferred_element_type=jnp.float32)
+
+
+def dot_nt(a, b):
+    return lax.dot_general(a, b, (((1,), (1,)), ((), ())), precision=HI, preferred_element_type=jnp.float32)
+
+
+def factor_block(d_ref, t_ref):
+    size = d_ref.shape[0]
+    steps = size // SUB
+    shape = (SUB, size)
+    lane = lax.broadcasted_iota(jnp.int32, shape, 1)
+    sub = lax.broadcasted_iota(jnp.int32, shape, 0)
+    rows = [d_ref[SUB * i : SUB * (i + 1), :] for i in range(steps)]
+    for p in range(steps):
+        base = SUB * p
+        pivot = (lane >= base) & (lane < base + SUB)
+        top = rows[p]
+        cols = [jnp.broadcast_to(top[:, base + s : base + s + 1], shape) for s in range(SUB)]
+        e = [[jnp.broadcast_to(cols[s][i : i + 1, :], shape) if s <= i else None for s in range(SUB)] for i in range(SUB)]
+        top = jnp.where(pivot, jnp.where(lane - base == sub, 1.0, 0.0), top)
+        u = [jnp.broadcast_to(top[s : s + 1, :], shape) for s in range(SUB)]
+        inv = [None] * SUB
+        for s in range(SUB):
+            inv[s] = lax.rsqrt(e[s][s])
+            u[s] = u[s] * inv[s]
+            for i in range(s + 1, SUB):
+                e[i][s] = e[i][s] * inv[s]
+            for q in range(s + 1, SUB):
+                for i in range(q, SUB):
+                    e[i][q] = e[i][q] - e[i][s] * e[q][s]
+                u[q] = u[q] - e[q][s] * u[s]
+        out = u[0]
+        for s in range(1, SUB):
+            out = jnp.where(sub == s, u[s], out)
+        t_ref[base : base + SUB, :] = jnp.where(lane <= base + sub, out, 0.0)
+        z = list(u)
+        for s in reversed(range(SUB)):
+            z[s] = z[s] * inv[s]
+            for q in range(s):
+                z[q] = z[q] - e[s][q] * z[s]
+        for i in range(p + 1, steps):
+            m = rows[i]
+            acc = jnp.where(pivot, 0.0, m)
+            for s in range(SUB):
+                acc = acc - jnp.broadcast_to(m[:, base + s : base + s + 1], shape) * z[s]
+            rows[i] = acc
+
+
+def inverse_kernel(a_ref, xh_ref, xl_ref, low, inv, work, block, tri):
+    order = a_ref.shape[0]
+    count = order // BLOCK
+
+    def store(r, c0, c1, value):
+        hi = value.astype(jnp.bfloat16)
+        xh_ref[r : r + BLOCK, c0:c1] = hi
+        xl_ref[r : r + BLOCK, c0:c1] = (value - hi.astype(jnp.float32)).astype(jnp.bfloat16)
+
+    def step(j, carry):
+        for jj in range(count):
+            at = BLOCK * jj
+
+            @pl.when(j == jj)
+            def _():
+                if jj == 0:
+                    work[...] = a_ref[:, :BLOCK]
+                    block[...] = a_ref[:BLOCK, :BLOCK]
+                else:
+                    got = a_ref[at:, at : at + BLOCK] - dot_nt(low[at:, :at], low[at : at + BLOCK, :at])
+                    work[at:, :] = got
+                    block[...] = got[:BLOCK, :]
+
+        factor_block(block, tri)
+        for jj in range(count):
+            at = BLOCK * jj
+
+            @pl.when(j == jj)
+            def _():
+                t = tri[...]
+                if jj + 1 < count:
+                    low[at + BLOCK :, at : at + BLOCK] = dot_nt(work[at + BLOCK :, :], t)
+                if jj:
+                    x = -dot_nn(t, dot_nn(low[at : at + BLOCK, :at], inv[:at, :at]))
+                    inv[at : at + BLOCK, :at] = x
+                    store(at, 0, at, x)
+                inv[at : at + BLOCK, at : at + BLOCK] = t
+                store(at, at, at + BLOCK, t)
+                if jj + 1 < count:
+                    inv[at : at + BLOCK, at + BLOCK :] = jnp.zeros((BLOCK, order - at - BLOCK), jnp.float32)
+                    xh_ref[at : at + BLOCK, at + BLOCK :] = jnp.zeros((BLOCK, order - at - BLOCK), jnp.bfloat16)
+                    xl_ref[at : at + BLOCK, at + BLOCK :] = jnp.zeros((BLOCK, order - at - BLOCK), jnp.bfloat16)
+
+        return carry
+
+    lax.fori_loop(0, count, step, 0)
+
+
+def inverse_of(tile):
+    order = tile.shape[0]
+    return pl.pallas_call(
+        inverse_kernel,
+        out_shape=[jax.ShapeDtypeStruct((order, order), jnp.bfloat16)] * 2,
+        in_specs=[pl.BlockSpec(memory_space=pltpu.VMEM)],
+        out_specs=[pl.BlockSpec(memory_space=pltpu.VMEM)] * 2,
+        scratch_shapes=[
+            pltpu.VMEM((order, order), jnp.float32),
+            pltpu.VMEM((order, order), jnp.float32),
+            pltpu.VMEM((order, BLOCK), jnp.float32),
+            pltpu.VMEM((BLOCK, BLOCK), jnp.float32),
+            pltpu.VMEM((BLOCK, BLOCK), jnp.float32),
+        ],
+        compiler_params=pltpu.CompilerParams(vmem_limit_bytes=40 * 2**20),
+        cost_estimate=pl.CostEstimate(flops=60 * 10**9, bytes_accessed=8 * order * order, transcendentals=0),
+    )(tile)
 
 
 def mask_columns(right, bucket):
@@ -11,26 +135,23 @@
     return jnp.where(live[None, :, :], right, jnp.zeros_like(right))
 
 
-def solve_whole(inverse, gathered):
-    flat = gathered.astype(jnp.float32).reshape(gathered.shape[0], -1)
-    solved = jnp.dot(
-        inverse, flat, precision=lax.Precision.HIGHEST, preferred_element_type=jnp.float32
+def solve_whole(high, low, gathered):
+    flat = gathered.reshape(gathered.shape[0], -1)
+    solved = jnp.dot(high, flat, preferred_element_type=jnp.float32) + jnp.dot(
+        low, flat, preferred_element_type=jnp.float32
     )
     return solved.astype(jnp.bfloat16).reshape(gathered.shape)
 
 
 def per_device(diag_tile, left_row, right_row, right_col, bucket_row, bucket_col):
     whole_tile = lax.all_gather(diag_tile, ("row", "col"), axis=0, tiled=True)
-    order = whole_tile.shape[0]
-    lower_factor = jnp.linalg.cholesky(whole_tile)
-    identity = jnp.eye(order, dtype=jnp.float32)
-    inverse = lax.linalg.triangular_solve(lower_factor, identity, left_side=True, lower=True)
+    high, low = inverse_of(whole_tile)
     masked_row = mask_columns(right_row, bucket_row)
     masked_col = mask_columns(right_col, bucket_col)
     row_position = lax.axis_index("col")
     col_position = lax.axis_index("row")
-    full_row = solve_whole(inverse, lax.all_gather(masked_row, "col", axis=0, tiled=True))
-    full_col = solve_whole(inverse, lax.all_gather(masked_col, "row", axis=0, tiled=True))
+    full_row = solve_whole(high, low, lax.all_gather(masked_row, "col", axis=0, tiled=True))
+    full_col = solve_whole(high, low, lax.all_gather(masked_col, "row", axis=0, tiled=True))
     panel_row = lax.dynamic_slice_in_dim(
         full_row, row_position * masked_row.shape[0], masked_row.shape[0], 0
     )

time: 525 us -> 234 us (0.45)
  other arithmetic: 270 us -> 5.37 us
  Pallas kernels: 0 us -> 53.3 us
  matrix products: 63.7 us -> 18.5 us
  local copies, waits for them, and re-layouts: 49.1 us -> 18.8 us
  between operations: 19.4 us -> 13.9 us
    another operation x33 -> x0, other arithmetic: 256 us -> none  [the longest x30 172 us: per_device(): lower_factor = jnp.linalg.cholesky(whole_tile)]
    pallas_call x0 -> x1, Pallas kernels: none -> 53.3 us  [inverse_of(): pl.pallas_call(inverse_kernel, out_shape=[jax.ShapeDtypeStruct((order, or...]
    another operation x29 -> x0, matrix products: 45.8 us -> none  [the longest x14 23 us: per_device(): lower_factor = jnp.linalg.cholesky(whole_tile)]
    another operation x33 -> x0, local copies, waits for them, and re-layouts: 25.6 us -> none
    all_gather x1 -> x0, local copies, waits for them, and re-layouts: 5.78 us -> none  [per_device(): whole_tile = lax.all_gather(diag_tile, ('row', 'col'), axis=0, tiled=True)]
    unnamed x12 -> x18, local copies, waits for them, and re-layouts: 16.6 us -> 18.6 us
    dot_general x2 -> x4, matrix products: 11.8 us -> 12.3 us  [the longest x2 6.6 us: solve_whole(): jnp.dot(low, flat, preferred_element_type=jnp.float32)]
  transfers between devices with their start and end apart: 4 -> 4, of which waited for: 3 -> 3; matrix products, arithmetic and copies ran while one was open for 69% -> 10% of each run, Pallas kernels for 0% -> 23%
where the time goes in v1:
time: 234 us
  waiting for transfers between devices  124 us (53%)
  Pallas kernels  53.3 us (23%)
  local copies, waits for them, and re-layouts  18.8 us (8%)
  matrix products  18.5 us (8%)
  between operations  13.9 us (6%)
  other arithmetic  5.37 us (2%)
    all_gather x1, waiting for transfers between devices, per_device(): whole_tile = lax.all_gather(diag_tile, ('row', 'col'), axis=0, tiled=True)  60 us
    pallas_call x1, Pallas kernels, inverse_of(): pl.pallas_call(inverse_kernel, out_shape=[jax.ShapeDtypeStruct((order, or...  53.3 us
    all_gather x1, waiting for transfers between devices, per_device(): lax.all_gather(masked_col, 'row', axis=0, tiled=True)  42.8 us
    all_gather x1, waiting for transfers between devices, per_device(): lax.all_gather(masked_row, 'col', axis=0, tiled=True)  20 us
    unnamed x18, local copies, waits for them, and re-layouts  18.6 us
    dot_general x2, matrix products, solve_whole(): jnp.dot(low, flat, preferred_element_type=jnp.float32)  6.6 us
    dot_general x1, matrix products, per_device(): jnp.einsum('kia,ijab->ijkb', lax.all_gather(left_row, 'col', axis=0, tile...  6.19 us
    dot_general x2, matrix products, solve_whole(): jnp.dot(high, flat, preferred_element_type=jnp.float32)  5.71 us
  transfers between devices with their start and end apart: 4, of which 3 were waited for; matrix products, arithmetic and copies ran while one was open for 10% of the time, Pallas kernels for 23%

profile of v1, /device:TPU:0, one launch (start us, length us, event | category | flops | bytes accessed | tf_op | source)
XLA Modules:
  0.0 233.5 jit_solution(7452998591337461866)
XLA Ops:
  7.2 0.0 all-gather.5.cloned.1.call-start
  7.2 0.7 broadcast_multiply_fusion.1
  7.9 0.1 iota_compare_fusion.1
  8.0 2.2 broadcast_select_fusion
  10.2 0.0 all-gather.5.cloned.1.call-update
  10.3 0.0 all-gather.9.cloned.1.call-start
  10.3 0.7 broadcast_multiply_fusion
  11.0 0.1 iota_compare_fusion
  11.1 1.6 broadcast_select_fusion.1
  12.7 0.0 all-gather.7.cloned.1.call-start
  12.7 0.7 all-gather.7.cloned.1.call-update
  13.4 0.0 all-gather.11.cloned.1.call-start
  13.5 0.9 copy.15
  14.4 20.0 %all-gather.5.cloned.1.call-done = bf16[1024,2,256]{2,1,0:T(2,128)(2,1)} async-done(((bf16[512,2,256]{2,1,0:T(2,128)(2,1)}), bf16[1024,2,256]{2,1,0:T(2,128)(2,1)}) %all-gather.5.cloned.1.call-update) | async-done | bytes 1048592 | tf_op jit(solution)/shard_map/all_gather | solution.py:153
  34.4 1.4 copy.21
  35.9 42.8 %all-gather.9.cloned.1.call-done = bf16[1024,4,256]{2,1,0:T(4,128)(2,1)} async-done(((bf16[64,4,256]{2,1,0:T(4,128)(2,1)}), bf16[1024,4,256]{2,1,0:T(4,128)(2,1)}) %all-gather.9.cloned.1.call-update) | async-done | bytes 2097168 | tf_op jit(solution)/shard_map/all_gather | solution.py:154
  78.7 3.4 %copy.22 = bf16[128,8,4,256]{3,1,2,0:T(8,128)(2,1)} copy(bf16[128,8,4,256]{3,2,1,0:T(4,128)(2,1)} %bitcast.37) | data formatting | bytes 4194304
  82.1 60.0 %all-gather.7.cloned.1.call-done.a_ref = f32[1024,1024]{1,0:T(8,128)} async-done(((f32[32,1024]{1,0:T(8,128)}), f32[1024,1024]{1,0:T(8,128)}) %all-gather.7.cloned.1.call-update) | async-done | bytes 4194320 | tf_op jit(solution)/shard_map/all_gather | solution.py:147
  142.1 2.2 copy-done
  144.3 53.3 %shard_map.85 = (bf16[1024,1024]{1,0:T(8,128)(2,1)S(1)}, bf16[1024,1024]{1,0:T(8,128)(2,1)S(1)}) custom-call(f32[1024,1024]{1,0:T(8,128)S(1)} %copy-done), custom_call_target="tpu_custom_call" | custom-call | flops 60000002048 | bytes 8388608 | tf_op jit(solution)/shard_map/pallas_call | solution.py:116
  197.6 1.3 fusion.3
  198.9 0.3 copy-done.1
  199.2 4.4 %fusion.4 = f32[1024,1024]{1,0:T(8,128)} fusion(bf16[1024,1024]{1,0:T(8,128)(2,1)S(1)} %bitcast.39, bf16[1024,1024]{1,0:T(8,128)(2,1)S(1)} %get-tuple-element.5), kind=kOutput, calls=%fused_computation.16 | convolution fusion | flops 2147483648 | bytes 8388608 | tf_op jit(solution)/shard_map/dot_general | solution.py:140
  203.6 1.3 add_convert_fusion.1
  205.0 1.0 copy-done.3
  206.0 1.1 copy.19
  207.1 5.3 %add_convert_fusion = bf16[1024,1024]{1,0:T(8,128)(2,1)S(1)} fusion(f32[1024,1024]{1,0:T(8,128)} %fusion.4, bf16[1024,1024]{1,0:T(8,128)(2,1)} %bitcast.38, bf16[1024,1024]{1,0:T(8,128)(2,1)S(1)} %get-tuple-element.6), kind=kOutput, calls=%fused_computation.2 | convolution fusion | flops 2149580800 | bytes 10485760 | tf_op jit(solution)/shard_map/dot_general | solution.py:140
  212.4 1.3 copy-done.5
  213.7 0.1 constant_dynamic-slice_fusion
  213.8 0.8 copy.20
  214.6 6.2 %fusion = bf16[2,4,1024,256]{2,3,1,0:T(8,128)(2,1)} fusion(bf16[1024,4,256,1]{0,2,1,3:T(8,128)(2,1)} %bitcast.46, bf16[1024,2,256,1]{0,2,3,1:T(8,128)(2,1)S(1)} %bitcast.44, bf16[1024,2,256]{2,0,1:T(8,128)(2,1)} %all-gather.11.cloned.1.call-done), kind=kOutput, calls=%fused_computation.1 | convolution fusion | flops 2152202240 | bytes 8388608 | tf_op jit(solution)/shard_map/kia,ijab->ijkb/dot_general | solution.py:164
  220.8 6.2 %copy.16 = bf16[2,4,1024,256]{3,2,1,0:T(8,128)(2,1)} copy(bf16[2,4,1024,256]{2,3,1,0:T(8,128)(2,1)} %fusion) | data formatting | bytes 8388608
  (12 shorter events, 0.1 us)
Async XLA Ops:
  7.2 6.3 %copy-start.2 = (bf16[512,2,256]{2,1,0:T(2,128)(2,1)S(1)}, bf16[512,2,256]{2,1,0:T(2,128)(2,1)}, u32[]{:S(2)}) copy-start(bf16[512,2,256]{2,1,0:T(2,128)(2,1)} %param.7) | copy-start | bytes 1572868
  7.2 27.3 %all-gather.5.cloned.1.call-start = ((), (), s32[]{:S(2)}) async-start(), calls=%async_computation | async-start | bytes 1572864 | tf_op jit(solution)/shard_map/all_gather | solution.py:153
  10.3 68.4 %all-gather.9.cloned.1.call-start = ((), (), s32[]{:S(2)}) async-start(), calls=%async_computation.2 | async-start | bytes 2228224 | tf_op jit(solution)/shard_map/all_gather | solution.py:154
  12.7 129.4 %all-gather.7.cloned.1.call-start = ((), (), s32[]{:S(2)}) async-start(), calls=%async_computation.1 | async-start | bytes 4325376 | tf_op jit(solution)/shard_map/all_gather | solution.py:147
  13.4 201.2 %all-gather.11.cloned.1.call-start = ((), (), s32[]{:S(2)}) async-start(), calls=%async_computation.3 | async-start | bytes 1572864 | tf_op jit(solution)/shard_map/all_gather | solution.py:166
  142.1 2.2 copy-start
  197.6 1.6 copy-start.1
  204.9 1.0 copy-start.3
  207.1 7.6 %copy-start.4 = (bf16[512,1024]{1,0:T(8,128)(2,1)S(1)}, bf16[512,1024]{1,0:T(8,128)(2,1)}, u32[]{:S(2)}) copy-start(bf16[512,1024]{1,0:T(8,128)(2,1)} %copy-done.3) | copy-start | bytes 3145732
  212.4 1.3 copy-start.5
Sparse Core Ops, SparseCore 0:
  10.4 23.9 all-gather.4
  37.2 41.4 all-gather.8
  81.7 60.4 all-gather.6
  143.5 20.0 all-gather.10

commit v2 on v1

--- a/solution.py
+++ b/solution.py
@@ -130,50 +130,187 @@
     )(tile)
 
 
+def gather_kernel(rows, cols, groups, x_ref, out_ref, send_sem, recv_sem):
+    order = out_ref.shape[2]
+    pairs = rows // groups // 2
+    row = lax.axis_index("row")
+    col = lax.axis_index("col")
+    group = row // (2 * pairs)
+    pair = (row // 2) % pairs
+    core = row % 2
+    offsets = [(a, b) for a in range(pairs) for b in range(cols)]
+
+    def device(g, p, c):
+        return {"row": (g * pairs + p) * 2 + core, "col": c}
+
+    def block(g, p, c, k):
+        return ((g * pairs + p) * 2 + k) * cols + c
+
+    def width(g):
+        return -(-order * (g + 1) // (groups * BLOCK)) * BLOCK
+
+    def copy(source, index, wide, sem, target):
+        return pltpu.make_async_remote_copy(
+            src_ref=source.at[:, :wide],
+            dst_ref=out_ref.at[index, :, :wide],
+            send_sem=send_sem.at[sem],
+            recv_sem=recv_sem.at[index],
+            device_id=target,
+            device_id_type=pl.DeviceIdType.MESH,
+        )
+
+    partner = {"row": (group * pairs + pair) * 2 + 1 - core, "col": col}
+    ring = [device((group + k) % groups, pair, col) for k in range(1, groups)]
+    plane = [device(group, (pair + a) % pairs, (col + b) % cols) for a, b in offsets[1:]]
+    barrier = pltpu.get_barrier_semaphore()
+    for peer in ring + plane + [partner]:
+        pl.semaphore_signal(barrier, inc=1, device_id=peer, device_id_type=pl.DeviceIdType.MESH)
+    pl.semaphore_wait(barrier, len(ring) + len(plane) + 1)
+
+    own = block(group, pair, col, core)
+    for g in range(groups):
+
+        @pl.when(group == g)
+        def _():
+            for k, peer in enumerate(ring):
+                copy(x_ref, own, width(g), k, peer).start()
+            for k, peer in enumerate(plane):
+                copy(x_ref, own, width(g), groups + g * len(offsets) + k, peer).start()
+            copy(x_ref, own, width(g), groups * (1 + len(offsets)) + g * len(offsets), partner).start()
+
+    out_ref[own] = x_ref[...]
+    for g in range(groups):
+
+        @pl.when(group != g)
+        def _():
+            index = block(g, pair, col, core)
+            got = out_ref.at[index]
+            copy(got, index, width(g), 0, partner).wait_recv()
+            for k, peer in enumerate(plane):
+                copy(got, index, width(g), groups + g * len(offsets) + k, peer).start()
+            copy(got, index, width(g), groups * (1 + len(offsets)) + g * len(offsets), partner).start()
+
+    for g in range(groups):
+        for n, (a, b) in enumerate(offsets):
+            if n:
+                index = block(g, (pair + a) % pairs, (col + b) % cols, core)
+                got = out_ref.at[index]
+                copy(got, index, width(g), 0, partner).wait_recv()
+                copy(got, index, width(g), groups * (1 + len(offsets)) + g * len(offsets) + n, partner).start()
+
+    for g in range(groups):
+        for n, (a, b) in enumerate(offsets):
+            index = block(g, (pair + a) % pairs, (col + b) % cols, 1 - core)
+            copy(out_ref.at[index], index, width(g), 0, partner).wait_recv()
+
+    for g in range(groups):
+
+        @pl.when(group == g)
+        def _():
+            for k, peer in enumerate(ring):
+                copy(x_ref, own, width(g), k, peer).wait_send()
+
+        for k, peer in enumerate(plane):
+            copy(x_ref, own, width(g), groups + g * len(offsets) + k, peer).wait_send()
+        for n in range(len(offsets)):
+            copy(x_ref, own, width(g), groups * (1 + len(offsets)) + g * len(offsets) + n, partner).wait_send()
+
+
+def gather_tile(part, rows, cols):
+    high, order = part.shape
+    groups = 4 if rows % 8 == 0 else 1
+    sends = groups * (1 + 2 * (rows // groups // 2) * cols)
+    blocks = pl.pallas_call(
+        functools.partial(gather_kernel, rows, cols, groups),
+        out_shape=jax.ShapeDtypeStruct((rows * cols, high, order), part.dtype),
+        in_specs=[pl.BlockSpec(memory_space=pltpu.VMEM)],
+        out_specs=pl.BlockSpec(memory_space=pltpu.VMEM),
+        scratch_shapes=[pltpu.SemaphoreType.DMA((sends,)), pltpu.SemaphoreType.DMA((rows * cols,))],
+        compiler_params=pltpu.CompilerParams(collective_id=0, has_side_effects=True),
+        cost_estimate=pl.CostEstimate(flops=20 * 10**9, bytes_accessed=4 * order * order, transcendentals=0),
+    )(part)
+    return blocks.reshape(order, order)
+
+
+def tail_kernel(xh_ref, xl_ref, v_ref, w_ref, u_ref, row_ref, col_ref, out_ref, coupling):
+    order = xh_ref.shape[0]
+    tiles = out_ref.shape[1]
+    rank = v_ref.shape[1]
+    chunk = 256
+
+    def solve(src, dst):
+        for at in range(0, order, chunk):
+            end = at + chunk
+            got = jnp.dot(xh_ref[at:end, :end], src[:end, :], preferred_element_type=jnp.float32)
+            got = got + jnp.dot(xl_ref[at:end, :end], src[:end, :], preferred_element_type=jnp.float32)
+            dst[at:end, :] = got.astype(jnp.bfloat16)
+
+    @pl.when(pl.program_id(0) == 0)
+    def _():
+        for j in range(tiles):
+            solve(w_ref.at[:, rank * j : rank * (j + 1)], col_ref.at[:, rank * j : rank * (j + 1)])
+
+    solve(v_ref, row_ref)
+    coupling[...] = lax.dot_general(
+        row_ref[...], col_ref[...], (((0,), (0,)), ((), ())), preferred_element_type=jnp.float32
+    ).astype(jnp.bfloat16)
+    for j in range(tiles):
+        for at in range(0, order, chunk):
+            got = jnp.dot(
+                u_ref[at : at + chunk, :], coupling[:, rank * j : rank * (j + 1)], preferred_element_type=jnp.float32
+            )
+            out_ref[0, j, at : at + chunk, :] = (-got).astype(jnp.bfloat16)
+
+
+def tail(high, low, v, w, u, rank):
+    order = high.shape[0]
+    count, tiles = v.shape[1] // rank, w.shape[1] // rank
+    whole = pl.BlockSpec((order, order), lambda i: (0, 0))
+    wide = pl.BlockSpec(w.shape, lambda i: (0, 0))
+    one = pl.BlockSpec((order, rank), lambda i: (0, i))
+    return pl.pallas_call(
+        tail_kernel,
+        grid=(count,),
+        out_shape=[
+            jax.ShapeDtypeStruct(v.shape, jnp.bfloat16),
+            jax.ShapeDtypeStruct(w.shape, jnp.bfloat16),
+            jax.ShapeDtypeStruct((count, tiles, order, rank), jnp.bfloat16),
+        ],
+        in_specs=[whole, whole, one, wide, one],
+        out_specs=[one, wide, pl.BlockSpec((1, tiles, order, rank), lambda i: (i, 0, 0, 0))],
+        scratch_shapes=[pltpu.VMEM((rank, w.shape[1]), jnp.bfloat16)],
+        compiler_params=pltpu.CompilerParams(vmem_limit_bytes=50 * 2**20),
+        cost_estimate=pl.CostEstimate(flops=8 * 10**9, bytes_accessed=18 * order * order, transcendentals=0),
+    )(high, low, v, w, u)
+
+
 def mask_columns(right, bucket):
     live = jnp.arange(right.shape[2], dtype=jnp.int32)[None, :] < (RSTEP * bucket)[:, None]
     return jnp.where(live[None, :, :], right, jnp.zeros_like(right))
 
 
-def solve_whole(high, low, gathered):
-    flat = gathered.reshape(gathered.shape[0], -1)
-    solved = jnp.dot(high, flat, preferred_element_type=jnp.float32) + jnp.dot(
-        low, flat, preferred_element_type=jnp.float32
-    )
-    return solved.astype(jnp.bfloat16).reshape(gathered.shape)
-
-
-def per_device(diag_tile, left_row, right_row, right_col, bucket_row, bucket_col):
-    whole_tile = lax.all_gather(diag_tile, ("row", "col"), axis=0, tiled=True)
-    high, low = inverse_of(whole_tile)
-    masked_row = mask_columns(right_row, bucket_row)
-    masked_col = mask_columns(right_col, bucket_col)
-    row_position = lax.axis_index("col")
-    col_position = lax.axis_index("row")
-    full_row = solve_whole(high, low, lax.all_gather(masked_row, "col", axis=0, tiled=True))
-    full_col = solve_whole(high, low, lax.all_gather(masked_col, "row", axis=0, tiled=True))
+def per_device(rows, cols, diag_tile, left_row, right_row, right_col, bucket_row, bucket_col):
+    rank = right_row.shape[2]
+    flat_row = mask_columns(right_row, bucket_row).reshape(right_row.shape[0], -1)
+    flat_col = mask_columns(right_col, bucket_col).reshape(right_col.shape[0], -1)
+    flat_left = left_row.reshape(left_row.shape[0], -1)
+    v = lax.all_gather(flat_row, "col", axis=0, tiled=True)
+    w = lax.all_gather(flat_col, "row", axis=0, tiled=True)
+    u = lax.all_gather(flat_left, "col", axis=0, tiled=True)
+    high, low = inverse_of(gather_tile(diag_tile, rows, cols))
+    full_row, full_col, update_left = tail(high, low, v, w, u, rank)
     panel_row = lax.dynamic_slice_in_dim(
-        full_row, row_position * masked_row.shape[0], masked_row.shape[0], 0
-    )
+        full_row, lax.axis_index("col") * flat_row.shape[0], flat_row.shape[0], 0
+    ).reshape(right_row.shape)
     panel_col = lax.dynamic_slice_in_dim(
-        full_col, col_position * masked_col.shape[0], masked_col.shape[0], 0
-    )
-    coupling = jnp.einsum(
-        "kia,kjb->ijab", full_row, full_col, preferred_element_type=jnp.float32
-    ).astype(jnp.bfloat16)
-    update = jnp.einsum(
-        "kia,ijab->ijkb",
-        lax.all_gather(left_row, "col", axis=0, tiled=True),
-        coupling,
-        preferred_element_type=jnp.float32,
-    )
-    update_left = (-update).astype(jnp.bfloat16)
+        full_col, lax.axis_index("row") * flat_col.shape[0], flat_col.shape[0], 0
+    ).reshape(right_col.shape)
     return (panel_row, panel_col, update_left)
 
 
 def solution(mesh):
     return jax.shard_map(
-        per_device,
+        functools.partial(per_device, mesh.shape["row"], mesh.shape["col"]),
         mesh=mesh,
         in_specs=(
             P(("row", "col"), None),

time: 234 us -> 136 us (0.58)
  waiting for transfers between devices: 124 us -> 1.91 us
  Pallas kernels: 53.3 us -> 105 us
  matrix products: 18.5 us -> 0 us
  local copies, waits for them, and re-layouts: 18.8 us -> 12.6 us
  other arithmetic: 5.37 us -> 2.4 us
    all_gather x4 -> x3, waiting for transfers between devices: 123 us -> 1.86 us  [the longest x1 1.85 us: per_device(): w = lax.all_gather(flat_col, 'row', axis=0, tiled=True)]
    pallas_call x0 -> x2, Pallas kernels: none -> 51.4 us  [the longest x1 39.1 us: gather_tile(): pl.pallas_call(functools.partial(gather_kernel, rows, cols, groups), out_...]
    dot_general x5 -> x0, matrix products: 18.5 us -> none  [the longest x2 6.6 us: solve_whole(): jnp.dot(low, flat, preferred_element_type=jnp.float32)]
    unnamed x18 -> x19, local copies, waits for them, and re-layouts: 18.6 us -> 9.98 us
  transfers between devices with their start and end apart: 4 -> 3, of which waited for: 3 -> 1; matrix products, arithmetic and copies ran while one was open for 10% -> 1% of each run, Pallas kernels for 23% -> 68%
where the time goes in v2:
time: 136 us; the launch traced here: 135 us
  Pallas kernels  105 us (77%)
  between operations  13.8 us (10%)
  local copies, waits for them, and re-layouts  12.6 us (9%)
  other arithmetic  2.4 us (2%)
  waiting for transfers between devices  1.91 us (1%)
    pallas_call x1, Pallas kernels, inverse_of(): pl.pallas_call(inverse_kernel, out_shape=[jax.ShapeDtypeStruct((order, or...  53.3 us
    pallas_call x1, Pallas kernels, gather_tile(): pl.pallas_call(functools.partial(gather_kernel, rows, cols, groups), out_...  39.1 us
    pallas_call x1, Pallas kernels, tail(): pl.pallas_call(tail_kernel, grid=(count,), out_shape=[jax.ShapeDtypeStruc...  12.2 us
    unnamed x19, local copies, waits for them, and re-layouts  9.98 us
  transfers between devices with their start and end apart: 3, of which 1 were waited for; matrix products, arithmetic and copies ran while one was open for 1% of the time, Pallas kernels for 68%

profile of v2, /device:TPU:0, one launch (start us, length us, event | category | flops | bytes accessed | tf_op | source)
XLA Modules:
  0.0 135.5 jit_solution(3842775967547569538)
XLA Ops:
  7.2 0.0 copy-start.5
  7.2 0.0 all-gather.4.cloned.1.call-start
  7.2 0.7 broadcast_multiply_fusion.1
  7.9 0.1 iota_compare_fusion.1
  8.0 1.5 %broadcast_select_fusion = bf16[512,2,256]{2,1,0:T(2,128)(2,1)S(1)} fusion(bf16[512,2,256]{2,1,0:T(2,128)(2,1)} %param.8, pred[2,256]{1,0:T(4,128)(4,1)S(1)} %iota_compare_fusion.1), kind=kLoop, calls=%fused_computation | loop fusion | flops 262144 | bytes 1049088 | tf_op jit(solution)/shard_map/jit(_where)/select_n | solution.py:289
  9.5 0.9 copy.9
  10.4 0.0 all-gather.4.cloned.1.call-update
  10.4 0.0 all-gather.8.cloned.1.call-start
  10.5 0.0 copy-done.5
  10.5 0.9 copy.11
  11.3 0.0 all-gather.8.cloned.1.call-update
  11.4 0.0 all-gather.6.cloned.1.call-start
  11.4 0.0 copy-done.7
  11.4 0.1 iota_compare_fusion
  11.5 0.0 copy-done.6
  11.5 0.1 broadcast_select_fusion.1
  11.6 0.7 copy.10
  12.2 0.0 all-gather.6.cloned.1.call-update
  12.3 39.1 %shard_map.85 = f32[32,32,1024]{2,1,0:T(8,128)} custom-call(f32[32,1024]{1,0:T(8,128)} %x_ref.1), custom_call_target="tpu_custom_call" | custom-call | flops 20000000000 | bytes 4194304 | tf_op jit(solution)/shard_map/pallas_call | solution.py:223
  51.4 0.0 copy-start.2
  51.4 2.4 %copy-done.2 = f32[32,32,1024]{2,1,0:T(8,128)S(1)} copy-done((f32[32,32,1024]{2,1,0:T(8,128)S(1)}, f32[32,32,1024]{2,1,0:T(8,128)}, u32[]{:S(2)}) %copy-start.2) | copy-done | bytes 4194328
  53.9 53.3 %shard_map.86 = (bf16[1024,1024]{1,0:T(8,128)(2,1)S(1)}, bf16[1024,1024]{1,0:T(8,128)(2,1)S(1)}) custom-call(f32[1024,1024]{1,0:T(8,128)S(1)} %bitcast.7), custom_call_target="tpu_custom_call" | custom-call | flops 60000002048 | bytes 8388608 | tf_op jit(solution)/shard_map/pallas_call | solution.py:116
  107.2 0.0 copy-start.3
  107.2 1.3 copy-done.3
  108.5 1.3 copy-done.4
  109.8 1.9 %all-gather.6.cloned.1.call-done.w_ref = bf16[1024,1024]{1,0:T(8,128)(2,1)} async-done(((bf16[64,1024]{1,0:T(8,128)(2,1)}), bf16[1024,1024]{1,0:T(8,128)(2,1)}) %all-gather.6.cloned.1.call-update) | async-done | bytes 2097168 | tf_op jit(solution)/shard_map/all_gather | solution.py:298
  111.7 1.2 copy-done
  112.9 1.2 copy-done.1
  114.1 12.2 %shard_map.87 = (bf16[1024,512]{1,0:T(8,128)(2,1)S(1)}, bf16[1024,1024]{1,0:T(8,128)(2,1)}, bf16[2,4,1024,256]{3,2,1,0:T(8,128)(2,1)}) custom-call(bf16[1024,1024]{1,0:T(8,128)(2,1)} %copy-done.3, bf16[1024,1024]{1,0:T(8,128)(2,1)} %copy-done.4, bf16[1024,512]{1,0:T(8,128)(2,1)S(1)} %copy-done, bf16[1024,1024]{1,0:T(8,128)(2,1)} %all-gather.6.cloned.1.call-done.w_ref, ...), custom_call_target="tpu_custom_call" | custom-call | flops 8000000000 | bytes 18874368 | tf_op jit(solution)/shard_map/pallas_call | solution.py:271
  126.4 0.9 reshape.64
  127.3 0.9 constant_dynamic-slice_fusion
  128.2 0.7 reshape.65
  (9 shorter events, 0.0 us)
Async XLA Ops:
  7.2 3.3 %copy-start.5 = (bf16[512,2,256]{2,1,0:T(2,128)(2,1)S(1)}, bf16[512,2,256]{2,1,0:T(2,128)(2,1)}, u32[]{:S(2)}) copy-start(bf16[512,2,256]{2,1,0:T(2,128)(2,1)} %param.7) | copy-start | bytes 1572868
  7.2 102.6 %all-gather.4.cloned.1.call-start = ((), (), s32[]{:S(2)}) async-start(), calls=%async_computation | async-start | bytes 1572864 | tf_op jit(solution)/shard_map/all_gather | solution.py:297
  8.0 3.4 %copy-start.7 = (s32[4]{0:T(128)S(1)}, s32[4]{0:T(128)}, u32[]{:S(2)}) copy-start(s32[4]{0:T(128)} %param.11) | copy-start | bytes 52
  8.0 3.5 %copy-start.6 = (bf16[64,4,256]{2,1,0:T(4,128)(2,1)S(1)}, bf16[64,4,256]{2,1,0:T(4,128)(2,1)}, u32[]{:S(2)}) copy-start(bf16[64,4,256]{2,1,0:T(4,128)(2,1)} %param.9) | copy-start | bytes 393220
  10.4 99.4 %all-gather.8.cloned.1.call-start = ((), (), s32[]{:S(2)}) async-start(), calls=%async_computation.2 | async-start | bytes 1572864 | tf_op jit(solution)/shard_map/all_gather | solution.py:299
  11.4 100.3 %all-gather.6.cloned.1.call-start = ((), (), s32[]{:S(2)}) async-start(), calls=%async_computation.1 | async-start | bytes 2228224 | tf_op jit(solution)/shard_map/all_gather | solution.py:298
  51.4 2.4 %copy-start.2 = (f32[32,32,1024]{2,1,0:T(8,128)S(1)}, f32[32,32,1024]{2,1,0:T(8,128)}, u32[]{:S(2)}) copy-start(f32[32,32,1024]{2,1,0:T(8,128)} %shard_map.85) | copy-start | bytes 12582916
  107.2 1.3 copy-start.3
  108.5 1.3 copy-start.4
  111.7 1.2 copy-start
  112.9 1.2 copy-start.1
Sparse Core Ops, SparseCore 0:
  10.5 31.4 all-gather.3
  44.1 23.1 all-gather.7
  70.1 41.5 all-gather.5

commit v3 on v2

--- a/solution.py
+++ b/solution.py
@@ -126,7 +126,7 @@
             pltpu.VMEM((BLOCK, BLOCK), jnp.float32),
         ],
         compiler_params=pltpu.CompilerParams(vmem_limit_bytes=40 * 2**20),
-        cost_estimate=pl.CostEstimate(flops=60 * 10**9, bytes_accessed=8 * order * order, transcendentals=0),
+        cost_estimate=pl.CostEstimate(flops=4 * 10**9, bytes_accessed=8 * order * order, transcendentals=0),
     )(tile)
 
 
@@ -227,7 +227,7 @@
         out_specs=pl.BlockSpec(memory_space=pltpu.VMEM),
         scratch_shapes=[pltpu.SemaphoreType.DMA((sends,)), pltpu.SemaphoreType.DMA((rows * cols,))],
         compiler_params=pltpu.CompilerParams(collective_id=0, has_side_effects=True),
-        cost_estimate=pl.CostEstimate(flops=20 * 10**9, bytes_accessed=4 * order * order, transcendentals=0),
+        cost_estimate=pl.CostEstimate(flops=60 * 10**9, bytes_accessed=4 * order * order, transcendentals=0),
     )(part)
     return blocks.reshape(order, order)
 
@@ -291,13 +291,16 @@
 
 def per_device(rows, cols, diag_tile, left_row, right_row, right_col, bucket_row, bucket_col):
     rank = right_row.shape[2]
+    flat_col = mask_columns(right_col, bucket_col).reshape(right_col.shape[0], -1)
+    flat_col, diag_tile = lax.optimization_barrier((flat_col, diag_tile))
+    w = lax.all_gather(flat_col, "row", axis=0, tiled=True)
+    whole_tile = gather_tile(diag_tile, rows, cols)
+    whole_tile, right_row, left_row = lax.optimization_barrier((whole_tile, right_row, left_row))
     flat_row = mask_columns(right_row, bucket_row).reshape(right_row.shape[0], -1)
-    flat_col = mask_columns(right_col, bucket_col).reshape(right_col.shape[0], -1)
     flat_left = left_row.reshape(left_row.shape[0], -1)
     v = lax.all_gather(flat_row, "col", axis=0, tiled=True)
-    w = lax.all_gather(flat_col, "row", axis=0, tiled=True)
     u = lax.all_gather(flat_left, "col", axis=0, tiled=True)
-    high, low = inverse_of(gather_tile(diag_tile, rows, cols))
+    high, low = inverse_of(whole_tile)
     full_row, full_col, update_left = tail(high, low, v, w, u, rank)
     panel_row = lax.dynamic_slice_in_dim(
         full_row, lax.axis_index("col") * flat_row.shape[0], flat_row.shape[0], 0

time: 136 us -> 154 us (1.13)
  waiting for transfers between devices: 1.91 us -> 28.5 us
  Pallas kernels: 105 us -> 96.8 us
    all_gather x1, waiting for transfers between devices: 1.85 us -> 27.8 us  [per_device(): w = lax.all_gather(flat_col, 'row', axis=0, tiled=True)]
    pallas_call x1, Pallas kernels: 39.1 us -> 31.2 us  [gather_tile(): pl.pallas_call(functools.partial(gather_kernel, rows, cols, groups), out_...]
  transfers between devices with their start and end apart: 3 -> 3, of which waited for: 1 -> 1; matrix products, arithmetic and copies ran while one was open for 1% -> 1% of each run, Pallas kernels for 68% -> 35%
where the time goes in v3:
time: 154 us
  Pallas kernels  96.8 us (63%)
  waiting for transfers between devices  28.5 us (19%)
  between operations  13.8 us (9%)
  local copies, waits for them, and re-layouts  12.3 us (8%)
  other arithmetic  2.18 us (1%)
    pallas_call x1, Pallas kernels, inverse_of(): pl.pallas_call(inverse_kernel, out_shape=[jax.ShapeDtypeStruct((order, or...  53.3 us
    pallas_call x1, Pallas kernels, gather_tile(): pl.pallas_call(functools.partial(gather_kernel, rows, cols, groups), out_...  31.2 us
    all_gather x1, waiting for transfers between devices, per_device(): w = lax.all_gather(flat_col, 'row', axis=0, tiled=True)  27.8 us
    pallas_call x1, Pallas kernels, tail(): pl.pallas_call(tail_kernel, grid=(count,), out_shape=[jax.ShapeDtypeStruc...  12.3 us
    unnamed x19, local copies, waits for them, and re-layouts  9.73 us
  transfers between devices with their start and end apart: 3, of which 1 were waited for; matrix products, arithmetic and copies ran while one was open for 1% of the time, Pallas kernels for 35%

profile of v3, /device:TPU:0, one launch (start us, length us, event | category | flops | bytes accessed | tf_op | source)
XLA Modules:
  0.0 153.8 jit_solution(5998003139547315035)
XLA Ops:
  7.2 0.0 all-gather.4.cloned.1.call-start
  7.2 0.7 broadcast_multiply_fusion.1
  7.9 0.1 iota_compare_fusion
  7.9 1.0 broadcast_select_fusion.1
  8.9 0.7 copy.9
  9.6 31.2 %shard_map.85 = f32[32,32,1024]{2,1,0:T(8,128)} custom-call(f32[32,1024]{1,0:T(8,128)} %x_ref), custom_call_target="tpu_custom_call" | custom-call | flops 60000002048 | bytes 4194304 | tf_op jit(solution)/shard_map/pallas_call | solution.py:223
  40.8 0.0 copy-start.6
  40.8 0.0 copy-done.7
  40.8 0.1 iota_compare_fusion.1
  40.9 0.0 copy-done.5
  40.9 0.4 broadcast_select_fusion
  41.3 0.9 copy.10
  42.2 0.0 all-gather.4.cloned.1.call-update
  42.2 0.0 all-gather.8.cloned.1.call-start
  42.3 0.0 copy-done.6
  42.3 0.9 copy.11
  43.2 0.0 all-gather.8.cloned.1.call-update
  43.2 0.0 all-gather.6.cloned.1.call-start
  43.3 0.7 all-gather.6.cloned.1.call-update
  43.9 0.0 copy-start.2
  44.0 2.2 %copy-done.2 = f32[32,32,1024]{2,1,0:T(8,128)S(1)} copy-done((f32[32,32,1024]{2,1,0:T(8,128)S(1)}, f32[32,32,1024]{2,1,0:T(8,128)}, u32[]{:S(2)}) %copy-start.2) | copy-done | bytes 4194328
  46.1 53.3 %shard_map.86 = (bf16[1024,1024]{1,0:T(8,128)(2,1)S(1)}, bf16[1024,1024]{1,0:T(8,128)(2,1)S(1)}) custom-call(f32[1024,1024]{1,0:T(8,128)S(1)} %bitcast.7), custom_call_target="tpu_custom_call" | custom-call | flops 4000000000 | bytes 8388608 | tf_op jit(solution)/shard_map/pallas_call | solution.py:116
  99.4 0.0 copy-start.3
  99.4 1.3 copy-done.3
  100.8 1.3 copy-done.4
  102.1 27.8 %all-gather.6.cloned.1.call-done.w_ref = bf16[1024,1024]{1,0:T(8,128)(2,1)} async-done(((bf16[64,1024]{1,0:T(8,128)(2,1)}), bf16[1024,1024]{1,0:T(8,128)(2,1)}) %all-gather.6.cloned.1.call-update) | async-done | bytes 2097168 | tf_op jit(solution)/shard_map/all_gather | solution.py:296
  129.9 1.2 copy-done
  131.1 1.2 copy-done.1
  132.4 12.3 %shard_map.87 = (bf16[1024,512]{1,0:T(8,128)(2,1)S(1)}, bf16[1024,1024]{1,0:T(8,128)(2,1)}, bf16[2,4,1024,256]{3,2,1,0:T(8,128)(2,1)}) custom-call(bf16[1024,1024]{1,0:T(8,128)(2,1)} %copy-done.3, bf16[1024,1024]{1,0:T(8,128)(2,1)} %copy-done.4, bf16[1024,512]{1,0:T(8,128)(2,1)S(1)} %copy-done, bf16[1024,1024]{1,0:T(8,128)(2,1)} %all-gather.6.cloned.1.call-done.w_ref, ...), custom_call_target="tpu_custom_call" | custom-call | flops 8000000000 | bytes 18874368 | tf_op jit(solution)/shard_map/pallas_call | solution.py:271
  144.7 0.9 reshape.64
  145.6 0.9 constant_dynamic-slice_fusion
  146.5 0.7 reshape.65
  (9 shorter events, 0.0 us)
Async XLA Ops:
  7.2 94.9 %all-gather.4.cloned.1.call-start = ((), (), s32[]{:S(2)}) async-start(), calls=%async_computation | async-start | bytes 1572864 | tf_op jit(solution)/shard_map/all_gather | solution.py:301
  9.6 31.2 %copy-start.7 = (s32[2]{0:T(128)S(1)}, s32[2]{0:T(128)}, u32[]{:S(2)}) copy-start(s32[2]{0:T(128)} %param.10) | copy-start | bytes 28
  9.6 31.3 %copy-start.5 = (bf16[512,2,256]{2,1,0:T(2,128)(2,1)S(1)}, bf16[512,2,256]{2,1,0:T(2,128)(2,1)}, u32[]{:S(2)}) copy-start(bf16[512,2,256]{2,1,0:T(2,128)(2,1)} %param.8) | copy-start | bytes 1572868
  40.8 1.5 copy-start.6
  42.2 59.9 %all-gather.8.cloned.1.call-start = ((), (), s32[]{:S(2)}) async-start(), calls=%async_computation.2 | async-start | bytes 1572864 | tf_op jit(solution)/shard_map/all_gather | solution.py:302
  43.2 86.7 %all-gather.6.cloned.1.call-start = ((), (), s32[]{:S(2)}) async-start(), calls=%async_computation.1 | async-start | bytes 2228224 | tf_op jit(solution)/shard_map/all_gather | solution.py:296
  43.9 2.2 %copy-start.2 = (f32[32,32,1024]{2,1,0:T(8,128)S(1)}, f32[32,32,1024]{2,1,0:T(8,128)}, u32[]{:S(2)}) copy-start(f32[32,32,1024]{2,1,0:T(8,128)} %shard_map.85) | copy-start | bytes 12582916
  99.4 1.3 copy-start.3
  100.8 1.3 copy-start.4
  129.9 1.2 copy-start
  131.1 1.2 copy-start.1
Sparse Core Ops, SparseCore 0:
  42.4 19.8 all-gather.3
  64.3 21.2 all-gather.7
  88.4 41.4 all-gather.5
